TPU v7x, 32 devices: a whole 2x2x4 slice. The times are simulated.
32 devices in a mesh: corpus: 16 (over z, y, x), tensor: 2 (over core).
Axes of the slice: x: 2, y: 2, z: 4, core: 2. Of those that a mesh axis runs over, the one named last changes fastest.
Arguments:
- q_states: bfloat16 [1024, 4096], P('corpus', 'tensor'), may hold values from -90 to 90
- k_states: bfloat16 [1024, 1024], P('corpus', 'tensor'), may hold values from -9 to 9
- v_states: bfloat16 [1024, 1024], P('corpus', 'tensor'), may hold values from -6 to 6
- residual: bfloat16 [1024, 4096], P('corpus'), may hold values from -170 to 170
- out_weight: bfloat16 [4096, 4096], P('tensor'), may hold values from -0.09375 to 0.09375
- final_gain: float32 [4096], replicated, may hold values from 0.25 to 1.75
- passages: bfloat16 [8192, 4096], P(('corpus', 'tensor')), may hold values from -5 to 5
- lengths: int32 [64], P('corpus'), may hold values from 1 to 16
Outputs:
- scores: float32 [64, 8192], P(None, ('corpus', 'tensor'))
- log_norm: float32 [64], replicated
All inputs are finite; a program needn't handle non-finite values.
Results may differ from a plain program's by a relative error of at most 0.0003.
The roundings to bfloat16 on the way count: a program that leaves them out, or rounds other values in their place, can miss the bound.
Values may be sent and summed in bfloat16 or wider, within the bound.
A program may use at most 64 MiB of HBM per device.

v0:
```python
import math

import jax
import jax.numpy as jnp
from jax import lax
from jax.sharding import PartitionSpec as P

HEAD_DIM = 128
SEQ = 16


score_scale = 50.0


def merged(value, axis, join):
    pieces = jax.tree.map(lambda part: lax.all_gather(part, axis), value)
    head = jax.tree.map(lambda part: part[0], pieces)
    tail = jax.tree.map(lambda part: part[1:], pieces)
    total, _ = lax.scan(lambda total, piece: (join(total, piece), None), head, tail)
    return total


def attend_last(queries, key_rows, value_rows, lengths):
    query_count = queries.shape[0]
    pair_heads = key_rows.shape[2] // HEAD_DIM
    grouped = queries.reshape(query_count, pair_heads, -1, HEAD_DIM)
    keyed = key_rows.reshape(query_count, SEQ, pair_heads, HEAD_DIM)
    valued = value_rows.reshape(query_count, SEQ, pair_heads, HEAD_DIM)
    logits = jnp.einsum(
        "bkgd,bskd->bkgs", grouped, keyed, preferred_element_type=jnp.float32
    ) / math.sqrt(HEAD_DIM)
    key_place = lax.broadcasted_iota(jnp.int32, (1, SEQ), 1)
    allowed = (key_place < lengths[:, None])[:, None, None, :]
    logits = jnp.where(allowed, logits, -1e30)
    highest = jnp.max(logits, axis=-1, keepdims=True)
    weights = jnp.where(allowed, jnp.exp(logits - highest), 0.0)
    attention = (weights / jnp.sum(weights, axis=-1, keepdims=True)).astype(jnp.bfloat16)
    context = jnp.einsum("bkgs,bskd->bkgd", attention, valued, preferred_element_type=jnp.float32)
    return context.reshape(query_count, -1).astype(jnp.bfloat16)


def normalize_rows(pooled, final_gain):
    scaled = pooled * final_gain[None, :]
    magnitude = jnp.maximum(jnp.sqrt(jnp.sum(scaled * scaled, axis=1, keepdims=True)), 1.0)
    return (scaled / magnitude).astype(jnp.bfloat16)


def on_device(q_states, k_states, v_states, residual, out_weight, final_gain, passages, lengths):
    query_count = lengths.shape[0]
    places = lax.broadcasted_iota(jnp.int32, (query_count, SEQ), 1)
    picked = (places == (lengths - 1)[:, None])[:, :, None]
    key_rows = k_states.reshape(query_count, SEQ, -1)
    value_rows = v_states.reshape(query_count, SEQ, -1)
    last_query = jnp.sum(
        jnp.where(picked, q_states.reshape(query_count, SEQ, -1).astype(jnp.float32), 0.0), axis=1
    ).astype(jnp.bfloat16)
    last_residual = jnp.sum(
        jnp.where(picked, residual.reshape(query_count, SEQ, -1).astype(jnp.float32), 0.0), axis=1
    )
    context = attend_last(last_query, key_rows, value_rows, lengths)
    partial_value = jnp.dot(context, out_weight, preferred_element_type=jnp.float32)
    pooled = last_residual + lax.psum(partial_value, "tensor")
    embed = normalize_rows(pooled, final_gain)
    scores = (
        lax.dot_general(
            lax.all_gather(embed, "corpus", axis=0, tiled=True),
            passages,
            (((1,), (1,)), ((), ())),
            preferred_element_type=jnp.float32,
        )
        * score_scale
    )
    local_peak = jnp.max(scores, axis=1)
    local_total = jnp.sum(jnp.exp(scores - local_peak[:, None]), axis=1)

    def combine(former, latter):
        highest = jnp.maximum(former[0], latter[0])
        return (
            highest,
            former[1] * jnp.exp(former[0] - highest) + latter[1] * jnp.exp(latter[0] - highest),
        )

    global_peak, global_total = merged((local_peak, local_total), ("corpus", "tensor"), combine)
    return (scores, global_peak + jnp.log(global_total))


def solution(mesh):
    in_specs = (
        P("corpus", "tensor"),
        P("corpus", "tensor"),
        P("corpus", "tensor"),
        P("corpus", None),
        P("tensor", None),
        P(),
        P(("corpus", "tensor"), None),
        P("corpus"),
    )
    out_specs = (P(None, ("corpus", "tensor")), P())
    return jax.shard_map(
        on_device, mesh=mesh, in_specs=in_specs, out_specs=out_specs, check_vma=False
    )
```

profile of v0, /device:TPU:0, one launch (start us, length us, event | category | flops | bytes accessed | tf_op | source)
XLA Modules:
  0.0 135.4 jit_solution(11040314828113501551)
XLA Ops:
  7.2 0.0 copy-start
  7.2 0.0 all-reduce.5.cloned.1.call-start
  7.2 0.9 iota_compare_fusion
  8.1 0.7 broadcast_add_fusion
  8.8 0.1 iota_compare_fusion.1
  8.9 1.1 fusion.11
  10.0 0.9 reshape_reshape.6
  10.9 0.1 fusion.9
  11.0 0.2 fusion.17
  11.2 0.9 reshape_reshape.7
  12.1 0.3 convolution_convert_fusion
  12.4 8.7 %fusion.19 = f32[4,4096]{1,0:T(4,128)} fusion(bf16[4,2048]{1,0:T(4,128)(2,1)S(1)} %convert_element_type.39, bf16[2048,4096]{1,0:T(8,128)(2,1)} %param.14), kind=kOutput, calls=%fused_computation.35 | convolution fusion | flops 67108864 | bytes 16859136 | tf_op jit(solution)/shard_map/dot_general | solution.py:61
  21.1 0.0 all-reduce.5.cloned.1.call-update
  21.1 0.0 copy-done.1
  21.1 0.3 fusion.10
  21.4 20.3 %all-reduce.5.cloned.1.call-done = f32[4,4096]{1,0:T(4,128)} async-done(((f32[4,4096]{1,0:T(4,128)}), f32[4,4096]{1,0:T(4,128)}) %all-reduce.5.cloned.1.call-update) | async-done | bytes 65552 | tf_op jit(solution)/shard_map/psum | solution.py:62
  41.7 1.0 multiply_reduce_fusion
  42.7 0.9 fusion.14
  43.7 44.1 %all-gather.2 = bf16[16,4,4096]{2,1,0:T(4,128)(2,1)S(1)} all-gather(bf16[1,4,4096]{2,1,0:T(4,128)(2,1)S(1)} %fusion.14), channel_id=1, replica_groups=mesh['corpus'=16,'tensor'=2] {'corpus'}, dimensions={0}, use_global_device_ids=true | all-gather | bytes 557056 | tf_op jit(solution)/shard_map/all_gather | solution.py:66
  87.7 0.1 reshape.76
  87.9 0.9 fusion.18
  88.7 0.0 copy-start.2
  88.7 0.2 exponential_reduce_fusion
  88.9 0.3 dynamic-update-slice
  89.2 0.3 dynamic-update-slice.1
  89.5 37.0 %all-reduce.2 = (f32[2048]{0:T(1024)S(1)}, f32[2048]{0:T(1024)S(1)}) all-reduce(f32[2048]{0:T(1024)S(1)} %dynamic-update-slice, f32[2048]{0:T(1024)S(1)} %dynamic-update-slice.1), channel_id=2, replica_groups=mesh['corpus'=16,'tensor'=2] {'corpus','tensor'}, use_global_device_ids=true, to_apply=%add | all-reduce | flops 4096 | bytes 32768
  126.5 0.1 slice.22
  126.5 0.1 slice.23
  126.6 0.1 reshape.69
  126.7 0.1 reshape.70
  126.8 1.3 while.12
  128.1 0.5 log_add_fusion
  (43 shorter events, 1.0 us)
Async XLA Ops:
  7.2 80.7 %copy-start = (bf16[256,4096]{1,0:T(8,128)(2,1)S(1)}, bf16[256,4096]{1,0:T(8,128)(2,1)}, u32[]{:S(2)}) copy-start(bf16[256,4096]{1,0:T(8,128)(2,1)} %param.16) | copy-start | bytes 6291460
  7.2 13.9 %copy-start.1 = (bf16[64,4096]{1,0:T(8,128)(2,1)S(1)}, bf16[64,4096]{1,0:T(8,128)(2,1)}, u32[]{:S(2)}) copy-start(bf16[64,4096]{1,0:T(8,128)(2,1)} %param.13) | copy-start | bytes 1572868
  7.2 34.5 %copy-start.3 = (f32[4096]{0:T(1024)S(1)}, f32[4096]{0:T(1024)}, u32[]{:S(2)}) copy-start(f32[4096]{0:T(1024)} %param.15) | copy-start | bytes 49156
  7.2 34.5 %all-reduce.5.cloned.1.call-start = ((), (), s32[]{:S(2)}) async-start(), calls=%async_computation | async-start | bytes 131072 | tf_op jit(solution)/shard_map/psum | solution.py:62
  88.7 39.9 %copy-start.2 = (f32[64,256]{1,0:T(8,128)}, f32[64,256]{1,0:T(8,128)S(1)}, u32[]{:S(2)}) copy-start(f32[64,256]{1,0:T(8,128)S(1)} %get-tuple-element.47) | copy-start | bytes 196612
Sparse Core Ops, SparseCore 0:
  21.2 20.4 all-reduce.4
where the time goes:
time: 136 us; the launch traced here: 135 us
  blocking collectives  81.1 us (60%)
  waiting for transfers between devices  20.3 us (15%)
  between operations  14.1 us (10%)
  matrix products  9.98 us (7%)
  other arithmetic  6.78 us (5%)
  local copies, waits for them, and re-layouts  2.73 us (2%)
    all_gather x1, blocking collectives, on_device(): lax.all_gather(embed, 'corpus', axis=0, tiled=True)  44.1 us
    unnamed x1, blocking collectives  37 us
    psum x1, waiting for transfers between devices, on_device(): pooled = last_residual + lax.psum(partial_value, 'tensor')  20.3 us
    dot_general x1, matrix products, on_device(): jnp.dot(context, out_weight, preferred_element_type=jnp.float32)  8.68 us
  transfers between devices with their start and end apart: 1, of which 1 were waited for; matrix products, arithmetic and copies ran while one was open for 0% of the time, Pallas kernels for 0%

commit v1 on v0

v1 whole, which is shorter than its diff:
```python
import functools
import math

import jax
import jax.numpy as jnp
from jax import lax
from jax.experimental import pallas as pl
from jax.experimental.pallas import tpu as pltpu
from jax.sharding import PartitionSpec as P

HEAD_DIM = 128
SEQ = 16
GROUP = 4
SCORE_SCALE = 50.0
F32 = jnp.float32
BF16 = jnp.bfloat16


def kernel(
    sizes, lengths, q_hbm, k_hbm, v_hbm, res_hbm, w_hbm, gain_hbm, pass_hbm,
    scores_hbm, norm_ref,
    q_ref, k_ref, v_ref, res_ref, w_ref, gain_ref, pass_ref,
    part, gathered, embed, scores_ref, pair_stat, all_stat,
    in_sem, w_sem, out_sem,
    part_send, part_recv, far_send, far_recv, near_send, near_recv, twin_send, twin_recv,
    pair_send, pair_recv, stat_send, stat_recv,
):
    corpus, tensor, group, chunks = sizes
    spans = corpus // group
    query_count = lengths.shape[0]
    rows = part.shape[2]
    key_count = k_ref.shape[0]
    kv_heads = k_ref.shape[1] // HEAD_DIM
    per_kv = q_ref.shape[1] // k_ref.shape[1]
    width = w_ref.shape[1]
    chunk = width // chunks
    share = width // tensor
    mine = lax.axis_index("corpus")
    twin = lax.axis_index("tensor")
    span = mine // group
    spot = lax.rem(mine, group)

    small = [(k_hbm, k_ref), (q_hbm, q_ref), (v_hbm, v_ref), (res_hbm, res_ref), (gain_hbm, gain_ref)]
    loads = [pltpu.make_async_copy(s, d, in_sem.at[i]) for i, (s, d) in enumerate(small)]
    pass_load = pltpu.make_async_copy(pass_hbm, pass_ref, in_sem.at[len(small)])
    for load in loads:
        load.start()
    w_loads = []
    for n in range(chunks):
        cols = pl.ds(n * chunk, chunk)
        w_loads.append(pltpu.make_async_copy(w_hbm.at[:, cols], w_ref.at[:, cols], w_sem.at[n]))
        w_loads[n].start()
    pass_load.start()

    def to(c, t):
        return dict(device_id=(c, t), device_id_type=pl.DeviceIdType.MESH)

    barrier = pltpu.get_barrier_semaphore()

    def greet(d, carry):
        pl.semaphore_signal(barrier, inc=1, **to(lax.rem(mine + d, corpus), twin))
        return carry

    lax.fori_loop(1, corpus, greet, 0)
    for d in range(1, tensor):
        pl.semaphore_signal(barrier, inc=1, **to(mine, lax.rem(twin + d, tensor)))

    row = lax.broadcasted_iota(jnp.int32, (rows, key_count), 0)
    col = lax.broadcasted_iota(jnp.int32, (rows, key_count), 1)
    picked = jnp.zeros((rows, key_count), jnp.bool_)
    allowed = jnp.zeros((rows, key_count), jnp.bool_)
    for b in range(query_count):
        length = lengths[b]
        picked = picked | ((row == b) & (col == b * SEQ + length - 1))
        allowed = allowed | ((row == b) & (col >= b * SEQ) & (col < b * SEQ + length))
    picker = jnp.where(picked, 1.0, 0.0).astype(BF16)
    allow = jnp.concatenate([jnp.where(allowed, 1.0, 0.0)] * per_kv, axis=0) > 0.5
    loads[0].wait()
    loads[1].wait()
    last_query = jnp.dot(picker, q_ref[...], preferred_element_type=F32)
    loads[2].wait()
    pieces = []
    for h in range(kv_heads):
        heads = slice(h * HEAD_DIM, (h + 1) * HEAD_DIM)
        stacked = jnp.concatenate(
            [last_query[:, (h * per_kv + g) * HEAD_DIM:(h * per_kv + g + 1) * HEAD_DIM]
             for g in range(per_kv)], axis=0).astype(BF16)
        logits = lax.dot_general(
            stacked, k_ref[:, heads], (((1,), (1,)), ((), ())), preferred_element_type=F32
        ) / math.sqrt(HEAD_DIM)
        logits = jnp.where(allow, logits, -1e30)
        highest = jnp.max(logits, axis=-1, keepdims=True)
        weights = jnp.where(allow, jnp.exp(logits - highest), 0.0)
        total = jnp.maximum(jnp.sum(weights, axis=-1, keepdims=True), 1.0)
        context = jnp.dot((weights / total).astype(BF16), v_ref[:, heads], preferred_element_type=F32)
        pieces += [context[g * rows:(g + 1) * rows] for g in range(per_kv)]
    context = jnp.concatenate(pieces, axis=1).astype(BF16)
    loads[3].wait()
    loads[4].wait()
    residual = jnp.dot(picker, res_ref[...], preferred_element_type=F32)

    pl.semaphore_wait(barrier, corpus - 1 + tensor - 1)

    sends = []
    for n in range(chunks):
        w_loads[n].wait()
        part[n, 0] = jnp.dot(context, w_ref[:, n * chunk:(n + 1) * chunk], preferred_element_type=F32)
        for d in range(1, tensor):
            send = pltpu.make_async_remote_copy(
                src_ref=part.at[n, 0], dst_ref=part.at[n, d],
                send_sem=part_send.at[n, d], recv_sem=part_recv.at[n, d],
                **to(mine, lax.rem(twin + d, tensor)))
            send.start()
            sends.append(send)
    scaled = []
    squares = 0.0
    for n in range(chunks):
        total = part[n, 0]
        for d in range(1, tensor):
            sends[n * (tensor - 1) + d - 1].wait_recv()
            total = total + part[n, d]
        cols = slice(n * chunk, (n + 1) * chunk)
        piece = (residual[:, cols] + total) * gain_ref[:, cols]
        squares = squares + jnp.sum(piece * piece, axis=1, keepdims=True)
        scaled.append(piece)
    magnitude = jnp.maximum(jnp.sqrt(squares), 1.0)
    per_share = chunks // tensor
    for n in range(chunks):
        inner = (n % per_share) * chunk
        gathered[n // per_share, mine, :, inner:inner + chunk] = (
            scaled[n] / magnitude)[:query_count].astype(BF16)

    def far(d, block):
        return pltpu.make_async_remote_copy(
            src_ref=gathered.at[twin, block], dst_ref=gathered.at[twin, block],
            send_sem=far_send.at[d], recv_sem=far_recv.at[d],
            **to(lax.rem(span + d, spans) * group + spot, twin))

    def near(d, g, block):
        return pltpu.make_async_remote_copy(
            src_ref=gathered.at[twin, block], dst_ref=gathered.at[twin, block],
            send_sem=near_send.at[d, g], recv_sem=near_recv.at[d, g],
            **to(span * group + lax.rem(spot + g, group), twin))

    def beside(d, g, t, owner, block):
        return pltpu.make_async_remote_copy(
            src_ref=gathered.at[owner, block], dst_ref=gathered.at[owner, block],
            send_sem=twin_send.at[d, g, t], recv_sem=twin_recv.at[d, g, t],
            **to(mine, lax.rem(twin + t, tensor)))

    def block_of(d, g):
        return lax.rem(span - d + spans, spans) * group + lax.rem(spot - g + group, group)

    def loop(low, high, body):
        def step(i, carry):
            body(i)
            return carry
        lax.fori_loop(low, high, step, 0)

    def start_far(d):
        far(d, mine).start()

    loop(1, spans, start_far)
    for g in range(1, group):
        near(0, g, mine).start()

    def relay(d):
        block = block_of(d, 0)
        far(d, block).wait_recv()
        for g in range(1, group):
            near(d, g, block).start()
        for t in range(1, tensor):
            beside(d, 0, t, twin, block).start()

    loop(1, spans, relay)

    def hand_over(d):
        for g in range(1, group):
            block = block_of(d, g)
            near(d, g, block).wait_recv()
            for t in range(1, tensor):
                beside(d, g, t, twin, block).start()

    loop(0, spans, hand_over)

    def take(d, g):
        for t in range(1, tensor):
            owner = lax.rem(twin - t + tensor, tensor)
            beside(d, g, t, owner, block_of(d, g)).wait_recv()

    def take_all(d):
        for g in range(group):
            take(d, g)

    for g in range(1, group):
        take(0, g)
    loop(1, spans, take_all)
    pass_load.wait()

    tile = 16 // query_count

    def assemble(i):
        for t in range(tensor):
            joined = jnp.concatenate(
                [gathered[t, i * tile + j].astype(F32) for j in range(tile)], axis=0)
            embed[pl.ds(pl.multiple_of(i * 16, 16), 16), t * share:(t + 1) * share] = joined.astype(BF16)

    loop(0, corpus // tile, assemble)
    scores = lax.dot_general(
        embed[...], pass_ref[...], (((1,), (1,)), ((), ())), preferred_element_type=F32
    ) * SCORE_SCALE
    scores_ref[...] = scores
    scores_out = pltpu.make_async_copy(scores_ref, scores_hbm, out_sem)
    scores_out.start()

    queries = scores.shape[0]
    padded = norm_ref.shape[1]
    peak = jnp.max(scores, axis=1, keepdims=True)
    total = jnp.sum(jnp.exp(scores - peak), axis=1, keepdims=True)
    lane = lax.broadcasted_iota(jnp.int32, (queries, 128), 1)
    both = jnp.where(lane == 0, peak, total)
    if padded > queries:
        both = jnp.concatenate([both, jnp.ones((padded - queries, 128), F32)], axis=0)
    pair_stat[0] = jnp.transpose(both)[:2]

    pair = [
        pltpu.make_async_remote_copy(
            src_ref=pair_stat.at[0], dst_ref=pair_stat.at[t],
            send_sem=pair_send.at[t], recv_sem=pair_recv.at[t],
            **to(mine, lax.rem(twin + t, tensor)))
        for t in range(1, tensor)
    ]
    for send in pair:
        send.start()
    for send in pair:
        send.wait_recv()

    def merge(stats):
        peaks, totals = stats[:, 0, :], stats[:, 1, :]
        high = jnp.max(peaks, axis=0, keepdims=True)
        return high, jnp.sum(totals * jnp.exp(peaks - high), axis=0, keepdims=True)

    high, total = merge(pair_stat[...])
    all_stat[mine] = jnp.concatenate([high, total], axis=0)

    def stat(d, block):
        return pltpu.make_async_remote_copy(
            src_ref=all_stat.at[block], dst_ref=all_stat.at[block],
            send_sem=stat_send.at[d], recv_sem=stat_recv.at[d],
            **to(lax.rem(mine + d, corpus), twin))

    loop(1, corpus, lambda d: stat(d, mine).start())
    for send in sends:
        send.wait_send()
    loop(1, spans, lambda d: far(d, mine).wait_send())

    def drain(d):
        for g in range(group):
            if g:
                near(d, g, block_of(d, 0)).wait_send()
            for t in range(1, tensor):
                beside(d, g, t, twin, block_of(d, g)).wait_send()

    for g in range(1, group):
        near(0, g, mine).wait_send()
        for t in range(1, tensor):
            beside(0, g, t, twin, block_of(0, g)).wait_send()
    loop(1, spans, drain)
    for send in pair:
        send.wait_send()
    scores_out.wait()
    loop(1, corpus, lambda d: stat(d, lax.rem(mine - d + corpus, corpus)).wait_recv())
    high, total = merge(all_stat[...])
    norm_ref[...] = high + jnp.log(total)
    loop(1, corpus, lambda d: stat(d, mine).wait_send())


def on_device(sizes, q_states, k_states, v_states, residual, out_weight, final_gain, passages, lengths):
    corpus, tensor, group, chunks = sizes
    query_count = lengths.shape[0]
    queries = query_count * corpus
    rows = -(-query_count // 8) * 8
    width = out_weight.shape[1]
    padded = -(-queries // 128) * 128
    spans = corpus // group
    local = passages.shape[0]
    hbm = pl.BlockSpec(memory_space=pl.ANY)
    dma = pltpu.SemaphoreType.DMA
    scores, norm = pl.pallas_call(
        functools.partial(kernel, sizes),
        out_shape=(
            jax.ShapeDtypeStruct((queries, local), F32),
            jax.ShapeDtypeStruct((1, padded), F32),
        ),
        in_specs=[pl.BlockSpec(memory_space=pltpu.SMEM)] + [hbm] * 7,
        out_specs=(hbm, pl.BlockSpec(memory_space=pltpu.VMEM)),
        scratch_shapes=[
            pltpu.VMEM(q_states.shape, BF16),
            pltpu.VMEM(k_states.shape, BF16),
            pltpu.VMEM(v_states.shape, BF16),
            pltpu.VMEM(residual.shape, BF16),
            pltpu.VMEM(out_weight.shape, BF16),
            pltpu.VMEM((1, width), F32),
            pltpu.VMEM(passages.shape, BF16),
            pltpu.VMEM((chunks, tensor, rows, width // chunks), F32),
            pltpu.VMEM((tensor, corpus, query_count, width // tensor), BF16),
            pltpu.VMEM((queries, width), BF16),
            pltpu.VMEM((queries, local), F32),
            pltpu.VMEM((tensor, 2, padded), F32),
            pltpu.VMEM((corpus, 2, padded), F32),
            dma((6,)), dma((chunks,)), dma,
            dma((chunks, tensor)), dma((chunks, tensor)),
            dma((spans,)), dma((spans,)),
            dma((spans, group)), dma((spans, group)),
            dma((spans, group, tensor)), dma((spans, group, tensor)),
            dma((tensor,)), dma((tensor,)),
            dma((corpus,)), dma((corpus,)),
        ],
        compiler_params=pltpu.CompilerParams(
            collective_id=0, has_side_effects=True, vmem_limit_bytes=60 * 1024 * 1024
        ),
    )(lengths, q_states, k_states, v_states, residual, out_weight, final_gain.reshape(1, -1), passages)
    return scores, norm[0, :queries]


def solution(mesh):
    corpus, tensor = mesh.shape["corpus"], mesh.shape["tensor"]
    group = GROUP if corpus % GROUP == 0 else 1
    sizes = (corpus, tensor, group, 4 * tensor)
    in_specs = (
        P("corpus", "tensor"),
        P("corpus", "tensor"),
        P("corpus", "tensor"),
        P("corpus", None),
        P("tensor", None),
        P(),
        P(("corpus", "tensor"), None),
        P("corpus"),
    )
    out_specs = (P(None, ("corpus", "tensor")), P())
    return jax.shard_map(
        functools.partial(on_device, sizes), mesh=mesh, in_specs=in_specs, out_specs=out_specs,
        check_vma=False,
    )
```

time: 136 us -> 32.9 us (0.24)
  blocking collectives: 81.1 us -> 0 us
  Pallas kernels: 0 us -> 29.5 us
  waiting for transfers between devices: 20.3 us -> 0 us
  between operations: 14.1 us -> 0.64 us
  matrix products: 9.98 us -> 0 us
  other arithmetic: 6.78 us -> 0 us
    all_gather x1 -> x0, blocking collectives: 44.1 us -> none  [on_device(): lax.all_gather(embed, 'corpus', axis=0, tiled=True)]
    unnamed x1 -> x0, blocking collectives: 37 us -> none
    pallas_call x0 -> x1, Pallas kernels: none -> 29.5 us  [on_device(): pl.pallas_call(functools.partial(kernel, sizes), out_shape=(jax.ShapeDtyp...]
    psum x1 -> x0, waiting for transfers between devices: 20.3 us -> none  [on_device(): pooled = last_residual + lax.psum(partial_value, 'tensor')]
    dot_general x4 -> x0, matrix products: 9.98 us -> none  [the longest x1 8.68 us: on_device(): jnp.dot(context, out_weight, preferred_element_type=jnp.float32)]
    reduce_sum x4 -> x0, other arithmetic: 2.61 us -> none  [the longest x1 1.14 us: on_device(): jnp.sum(jnp.where(picked, q_states.reshape(query_count, SEQ, -1).astype(j...]
    another operation x2 -> x0, local copies, waits for them, and re-layouts: 1.73 us -> none  [the longest x1 0.86 us: attend_last(): valued = value_rows.reshape(query_count, SEQ, pair_heads, HEAD_DIM)]
    add x32 -> x0, other arithmetic: 1.43 us -> none  [the longest x31 0.91 us: combine(): former[1] * jnp.exp(former[0] - highest)]
  transfers between devices with their start and end apart: 1 -> 0, of which waited for: 1 -> 0; matrix products, arithmetic and copies ran while one was open for 0% -> 0% of each run, Pallas kernels for 0% -> 0%
where the time goes in v1:
time: 32.9 us; the launch traced here: 32.7 us
  Pallas kernels  29.5 us (90%)
  local copies, waits for them, and re-layouts  2.59 us (8%)
  between operations  0.64 us (2%)
    pallas_call x1, Pallas kernels, on_device(): pl.pallas_call(functools.partial(kernel, sizes), out_shape=(jax.ShapeDtyp...  29.5 us
    unnamed x1, local copies, waits for them, and re-layouts  1.47 us
    squeeze x1, local copies, waits for them, and re-layouts, on_device(): return (scores, norm[0, :queries])  1.12 us

profile of v1, /device:TPU:0, one launch (start us, length us, event | category | flops | bytes accessed | tf_op | source)
XLA Modules:
  0.0 32.7 jit_solution(11887267335945455497)
XLA Ops:
  0.6 29.5 %shard_map.95 = (f32[64,256]{1,0:T(8,128)}, f32[1,128]{1,0:T(1,128)}) custom-call(s32[4]{0:T(128)} %lengths.1, bf16[64,2048]{1,0:T(8,128)(2,1)} %q_hbm.1, bf16[64,512]{1,0:T(8,128)(2,1)} %k_hbm.1, bf16[64,512]{1,0:T(8,128)(2,1)} %v_hbm.1, bf16[64,4096]{1,0:T(8,128)(2,1)} %res_hbm.1, bf16[2048,4096]{1,0:T(8,128)(2,1)} %w_hbm.1, f32[1,4096]{1,0:T(1,128)} %bitcast.3, ...), custom_call_target="tpu_custom_call" | custom-call | tf_op jit(solution)/shard_map/pallas_call | solution.py:289
  30.1 1.1 %slice_bitcast_fusion = f32[64]{0:T(128)} fusion(f32[1,128]{1,0:T(1,128)} %get-tuple-element.5), kind=kLoop, calls=%fused_computation | loop fusion | bytes 512 | tf_op jit(solution)/shard_map/squeeze | solution.py:323
  31.2 1.5 %copy.11 = f32[64,256]{1,0:T(8,128)} copy(f32[64,256]{1,0:T(8,128)} %get-tuple-element.8) | data formatting | bytes 131072
